TPU v7x, 32 devices: a whole 2x2x4 slice. The times are simulated.
32 devices in a mesh: rep: 2 (over core), tab: 16 (over z, y, x).
Axes of the slice: x: 2, y: 2, z: 4, core: 2. Of those that a mesh axis runs over, the one named last changes fastest.
Arguments:
- grad_out: bfloat16 [8192, 16, 128], P(('rep', 'tab')), may hold values from -1.5 to 1.5
- indices: int32 [16, 8192], P('tab', 'rep'), may hold values from 0 to 1023
- projections: bfloat16 [16, 128, 128], P('tab'), may hold values from -0.75 to 0.75
- widths: int32 [16], replicated, may hold values from 16 to 128
- hot_ids: int32 [16, 32], P('tab'), may hold values from 0 to 1023, as said below
Outputs:
- cold_grad: float32 [2, 16, 1024, 128], P('rep', 'tab')
- hot_grad: float32 [16, 32, 128], P('tab', 'rep')
Inputs may be any that keep to these rules, and one draw needn't show every extreme that they name: `hot_ids`: the 32 hot rows of one table are distinct.
All inputs are finite; a program needn't handle non-finite values.
Results may differ from a plain program's by a relative error of at most 0.005.
Values may be sent and summed in bfloat16 or wider, within the bound.
No kernel may reach another device: no remote copies, remote signals or barrier semaphores. Data moves between devices by JAX's collectives and lax.ppermute only.
A program may use at most 128 MiB of HBM per device.

v0:
```python
import math
import jax
import jax.numpy as jnp
from jax import lax
from jax.sharding import PartitionSpec as P

ROWS = 1024


def swapped(block, axis, bit):
    count = lax.axis_size(axis)
    route = []
    for low in range(count):
        high = low | 1 << bit
        if high != low and high < count:
            route += [(low, high), (high, low)]
    return lax.ppermute(block, axis, route)


def block_sums(narrow_rows, lookups):
    total_len = narrow_rows.shape[0]
    block_len = math.gcd(total_len, 4096)
    turn_count = total_len // block_len
    positions = lax.broadcasted_iota(jnp.int32, (1, ROWS), 1)

    def add_block(block, totals):
        piece_rows = lax.dynamic_slice_in_dim(narrow_rows, block * block_len, block_len, 0)
        row_ids = lax.dynamic_slice_in_dim(lookups, block * block_len, block_len, 0)
        onehot = (row_ids[:, None] == positions).astype(jnp.bfloat16)
        return totals + lax.dot_general(
            onehot, piece_rows, (((0,), (0,)), ((), ())), preferred_element_type=jnp.float32
        )

    start_sums = jnp.zeros((ROWS, narrow_rows.shape[1]), jnp.float32)
    return lax.fori_loop(0, turn_count, add_block, start_sums)


def shards(grad_out, indices, projections, widths, hot_ids):
    tab_dev = projections.shape[0]
    base_width = projections.shape[2]
    columns = lax.broadcasted_iota(jnp.int32, (1, 1, base_width), 2)
    first_table = lax.axis_index("tab") * tab_dev
    own_widths = lax.dynamic_slice_in_dim(widths, first_table, tab_dev, 0)
    received = lax.all_to_all(grad_out, "tab", split_axis=1, concat_axis=0, tiled=True)
    full_proj = jnp.einsum(
        "bte,tej->tbj", received, projections, preferred_element_type=jnp.float32
    )
    narrow = jnp.where(columns < own_widths[:, None, None], full_proj, 0.0).astype(jnp.bfloat16)
    table_grads = [block_sums(narrow[0], indices[0])]
    row_grads = jnp.stack(table_grads)
    own_hot = jnp.take_along_axis(row_grads, hot_ids[:, :, None], axis=1)
    half_hot = hot_ids.shape[1] // 2
    replica = lax.axis_index("rep")
    kept_rows = lax.dynamic_slice_in_dim(own_hot, replica * half_hot, half_hot, 1)
    given_rows = lax.dynamic_slice_in_dim(own_hot, (1 - replica) * half_hot, half_hot, 1)
    partner = swapped(given_rows, "rep", 0)
    hot_grad = kept_rows + partner
    all_rows = lax.broadcasted_iota(jnp.int32, (1, 1, ROWS), 2)
    is_hot = jnp.any(hot_ids[:, :, None] == all_rows, axis=1)
    cold_grad = jnp.where(is_hot[:, :, None], jnp.float32(0.0), row_grads)
    return (cold_grad[None], hot_grad)


def solution(mesh):
    placed = (
        P(("rep", "tab"), None, None),
        P("tab", "rep"),
        P("tab", None, None),
        P(),
        P("tab", None),
    )
    return jax.shard_map(
        shards,
        mesh=mesh,
        in_specs=placed,
        out_specs=(P("rep", "tab", None, None), P("tab", "rep", None)),
        check_vma=False,
    )
```

profile of v0, /device:TPU:9, one launch (start us, length us, event | category | flops | bytes accessed | tf_op | source)
XLA Modules:
  0.0 44.1 jit_solution(15511810765626345854)
XLA Ops:
  0.6 0.0 copy-start
  0.6 2.5 %copy.8 = bf16[256,16,128]{2,0,1:T(8,128)(2,1)} copy(bf16[256,16,128]{2,1,0:T(8,128)(2,1)} %param.5) | data formatting | bytes 2097152 | tf_op args[0]
  3.1 0.0 copy-start.2
  3.1 0.0 copy-start.3
  3.1 0.0 copy-start.1
  3.1 6.8 %all-to-all-start = ((bf16[256,16,128]{2,0,1:T(8,128)(2,1)}), bf16[256,16,128]{2,0,1:T(8,128)(2,1)S(1)}, u32[]{:S(2)}, u32[]{:S(2)}) async-start(bf16[256,16,128]{2,0,1:T(8,128)(2,1)} %copy.8), calls=%async_computation | async-start | bytes 2097152 | tf_op jit(solution)/shard_map/all_to_all | solution.py:44
  9.9 0.0 copy-done.2
  9.9 0.6 %dynamic_slice.13 = s32[1]{0:T(128)} dynamic-slice(s32[16]{0:T(128)S(1)} %copy-done.2, s32[]{:T(128)S(6)} %select_n.55), dynamic_slice_sizes={1} | dynamic-slice | bytes 12 | tf_op jit(solution)/shard_map/dynamic_slice | solution.py:43
  10.5 0.6 %iota_compare_fusion.3 = pred[128]{0:T(512)(128)(4,1)S(1)} fusion(s32[]{:T(128)} %bitcast.2), kind=kLoop, calls=%fused_computation.20 | loop fusion | flops 128 | bytes 132 | tf_op jit(solution)/shard_map/lt | solution.py:48
  11.2 0.0 copy-done.3
  11.2 0.1 fusion.5
  11.3 23.0 %all-to-all-done = bf16[256,16,128]{2,0,1:T(8,128)(2,1)S(1)} async-done(((bf16[256,16,128]{2,0,1:T(8,128)(2,1)}), bf16[256,16,128]{2,0,1:T(8,128)(2,1)S(1)}, u32[]{:S(2)}, u32[]{:S(2)}) %all-to-all-start) | async-done | bytes 1048608 | tf_op jit(solution)/shard_map/all_to_all | solution.py:44
  34.3 0.0 copy-done
  34.3 0.0 copy-done.1
  34.3 5.1 %fusion = f32[1024,128]{1,0:T(8,128)S(1)} fusion(s32[4096]{0:T(1024)S(1)} %bitcast.23, bf16[4096,128]{1,0:T(8,128)(2,1)S(1)} %bitcast.22, pred[128]{0:T(512)(128)(4,1)S(1)} %iota_compare_fusion.3, bf16[1,128,128]{2,1,0:T(8,128)(2,1)S(1)} %copy-done), kind=kOutput, calls=%fused_computation.2 | convolution fusion | flops 1213202432 | bytes 1622144 | tf_op jit(solution)/shard_map/while/body/eval_jaxpr/dot_general | solution.py:30
  39.4 0.6 %gather_fusion = f32[32,128]{1,0:T(8,128)S(1)} fusion(f32[1024,128]{1,0:T(8,128)S(1)} %fusion, s32[1024]{0:T(1024)S(1)} %pad_clamp_fusion), kind=kCustom, calls=%fused_computation | custom fusion | bytes 32896 | tf_op jit(solution)/shard_map/jit(take_along_axis)/gather | solution.py:51
  40.0 0.1 bitcast_select_fusion
  40.1 2.4 %collective-permute-start = (f32[1,16,128]{2,1,0:T(8,128)S(1)}, f32[1,16,128]{2,1,0:T(8,128)S(1)}, u32[]{:S(2)}, u32[]{:S(2)}) collective-permute-start(f32[1,16,128]{2,1,0:T(8,128)S(1)} %constant_dynamic-slice_fusion), channel_id=1, source_target_pairs={{0,16},{16,0},{1,17},{17,1},{2,18},{18,2},{3,19},{19,3},{4,20},{20... | collective-permute-start | bytes 24584 | tf_op jit(solution)/shard_map/ppermute | solution.py:17
  42.5 1.0 %select_bitcast_fusion = f32[1,1,1024,128]{3,2,1,0:T(8,128)} fusion(f32[1024,128]{1,0:T(8,128)S(1)} %fusion, pred[1024]{0:T(1024)(128)(4,1)S(1)} %fusion.5), kind=kLoop, calls=%fused_computation.8 | loop fusion | flops 131072 | bytes 1049600 | tf_op jit(solution)/shard_map/broadcast_in_dim | solution.py:61
  43.5 0.0 collective-permute-done
  43.5 0.6 %dynamic-slice_add_fusion = f32[1,16,128]{2,1,0:T(8,128)} fusion(f32[1,16,128]{2,1,0:T(8,128)S(1)} %collective-permute-done, f32[1,32,128]{2,1,0:T(8,128)S(1)} %bitcast_select_fusion, s32[]{:T(128)S(6)} %select_n.61), kind=kLoop, calls=%fused_computation.13 | loop fusion | flops 2048 | bytes 24580 | tf_op jit(solution)/shard_map/add | solution.py:57
  (4 shorter events, 0.0 us)
Async XLA Ops:
  0.6 33.7 %copy-start = (bf16[1,128,128]{2,1,0:T(8,128)(2,1)S(1)}, bf16[1,128,128]{2,1,0:T(8,128)(2,1)}, u32[]{:S(2)}) copy-start(bf16[1,128,128]{2,1,0:T(8,128)(2,1)} %param.7) | copy-start | bytes 98308
  3.1 6.8 %copy-start.2 = (s32[16]{0:T(128)S(1)}, s32[16]{0:T(128)}, u32[]{:S(2)}) copy-start(s32[16]{0:T(128)} %param.8) | copy-start | bytes 196
  3.1 8.1 %copy-start.3 = (s32[1,32]{1,0:T(1,128)S(1)}, s32[1,32]{1,0:T(1,128)}, u32[]{:S(2)}) copy-start(s32[1,32]{1,0:T(1,128)} %param.9) | copy-start | bytes 388
  3.1 31.2 %copy-start.1 = (s32[1,4096]{1,0:T(1,128)S(1)}, s32[1,4096]{1,0:T(1,128)}, u32[]{:S(2)}) copy-start(s32[1,4096]{1,0:T(1,128)} %param.6) | copy-start | bytes 49156
  3.1 31.2 %all-to-all-start = ((bf16[256,16,128]{2,0,1:T(8,128)(2,1)}), bf16[256,16,128]{2,0,1:T(8,128)(2,1)S(1)}, u32[]{:S(2)}, u32[]{:S(2)}) async-start(bf16[256,16,128]{2,0,1:T(8,128)(2,1)} %copy.8), calls=%async_computation | async-start | bytes 2097152 | tf_op jit(solution)/shard_map/all_to_all | solution.py:44
  40.1 3.4 %collective-permute-start = (f32[1,16,128]{2,1,0:T(8,128)S(1)}, f32[1,16,128]{2,1,0:T(8,128)S(1)}, u32[]{:S(2)}, u32[]{:S(2)}) collective-permute-start(f32[1,16,128]{2,1,0:T(8,128)S(1)} %constant_dynamic-slice_fusion), channel_id=1, source_target_pairs={{0,16},{16,0},{1,17},{17,1},{2,18},{18,2},{3,19},{19,3},{4,20},{20... | collective-permute-start | bytes 24584 | tf_op jit(solution)/shard_map/ppermute | solution.py:17
where the time goes:
time: 44.4 us; the launch traced here: 44.1 us
  waiting for transfers between devices  23 us (52%)
  starting transfers between devices  9.21 us (21%)
  matrix products  5.13 us (12%)
  local copies, waits for them, and re-layouts  3.65 us (8%)
  other arithmetic  2.44 us (5%)
  between operations  0.69 us (2%)
    all_to_all x1, waiting for transfers between devices, shards(): lax.all_to_all(grad_out, 'tab', split_axis=1, concat_axis=0, tiled=True)  23 us
    all_to_all x1, starting transfers between devices, shards(): lax.all_to_all(grad_out, 'tab', split_axis=1, concat_axis=0, tiled=True)  6.8 us
    dot_general x1, matrix products, add_block(): lax.dot_general(onehot, piece_rows, (((0,), (0,)), ((), ())), preferred_e...  5.13 us
    unnamed x9, local copies, waits for them, and re-layouts  2.49 us
    ppermute x1, starting transfers between devices, swapped(): return lax.ppermute(block, axis, route)  2.41 us
    broadcast_in_dim x1, other arithmetic, shards(): return (cold_grad[None], hot_grad)  1 us
  transfers between devices with their start and end apart: 2, of which 1 were waited for; matrix products, arithmetic and copies ran while one was open for 5% of the time, Pallas kernels for 0%

commit v1 on v0

--- a/solution.py
+++ b/solution.py
@@ -41,7 +41,10 @@
     columns = lax.broadcasted_iota(jnp.int32, (1, 1, base_width), 2)
     first_table = lax.axis_index("tab") * tab_dev
     own_widths = lax.dynamic_slice_in_dim(widths, first_table, tab_dev, 0)
-    received = lax.all_to_all(grad_out, "tab", split_axis=1, concat_axis=0, tiled=True)
+    received = jnp.concatenate(
+        lax.all_to_all(jnp.stack(jnp.split(grad_out, lax.axis_size("tab"), axis=1)), "tab", 0, 0),
+        axis=0,
+    )
     full_proj = jnp.einsum(
         "bte,tej->tbj", received, projections, preferred_element_type=jnp.float32
     )

time: 44.4 us -> 58.3 us (1.31)
  local copies, waits for them, and re-layouts: 3.65 us -> 17.6 us
    unnamed x9 -> x23, local copies, waits for them, and re-layouts: 2.49 us -> 9.46 us
    split x0 -> x1, local copies, waits for them, and re-layouts: none -> 6.32 us  [shards(): jnp.split(grad_out, lax.axis_size('tab'), axis=1)]
    another operation x0 -> x1, local copies, waits for them, and re-layouts: none -> 0.64 us  [shards(): jnp.stack(jnp.split(grad_out, lax.axis_size('tab'), axis=1))]
  transfers between devices with their start and end apart: 2 -> 2, of which waited for: 1 -> 1; matrix products, arithmetic and copies ran while one was open for 5% -> 4% of each run, Pallas kernels for 0% -> 0%
where the time goes in v1:
time: 58.3 us; the launch traced here: 58.1 us
  waiting for transfers between devices  23 us (39%)
  local copies, waits for them, and re-layouts  17.6 us (30%)
  starting transfers between devices  9.21 us (16%)
  matrix products  5.13 us (9%)
  other arithmetic  2.44 us (4%)
  between operations  0.7 us (1%)
    all_to_all x1, waiting for transfers between devices, shards(): lax.all_to_all(jnp.stack(jnp.split(grad_out, lax.axis_size('tab'), axis=1...  23 us
    unnamed x23, local copies, waits for them, and re-layouts  9.46 us
    all_to_all x1, starting transfers between devices, shards(): lax.all_to_all(jnp.stack(jnp.split(grad_out, lax.axis_size('tab'), axis=1...  6.8 us
    split x1, local copies, waits for them, and re-layouts, shards(): jnp.split(grad_out, lax.axis_size('tab'), axis=1)  6.32 us
    dot_general x1, matrix products, add_block(): lax.dot_general(onehot, piece_rows, (((0,), (0,)), ((), ())), preferred_e...  5.13 us
    ppermute x1, starting transfers between devices, swapped(): return lax.ppermute(block, axis, route)  2.41 us
  transfers between devices with their start and end apart: 2, of which 1 were waited for; matrix products, arithmetic and copies ran while one was open for 4% of the time, Pallas kernels for 0%

profile of v1, /device:TPU:9, one launch (start us, length us, event | category | flops | bytes accessed | tf_op | source)
XLA Modules:
  0.0 58.1 jit_solution(6389287765299000777)
XLA Ops:
  0.6 0.0 copy-start
  0.6 6.3 %fusion.26 = (bf16[256,1,128]{2,1,0:T(2,128)(2,1)S(1)}, bf16[256,1,128]{2,1,0:T(2,128)(2,1)S(1)}, bf16[256,1,128]{2,1,0:T(2,128)(2,1)S(1)}, bf16[256,1,128]{2,1,...) fusion(bf16[256,16,128]{2,1,0:T(8,128)(2,1)} %param.5), kind=kLoop, calls=%fused_computation.54 | loop fusion | bytes 2097152 | tf_op jit(solution)/shard_map/split | solution.py:45
  7.0 0.6 %fusion.21 = bf16[16,256,1,128]{3,1,2,0:T(8,128)(2,1)} fusion(bf16[256,1,128]{2,1,0:T(2,128)(2,1)S(1)} %get-tuple-element.35), kind=kLoop, calls=%fused_computation.42 | loop fusion | bytes 131072
  7.6 0.6 %fusion.20 = bf16[16,256,1,128]{3,1,2,0:T(8,128)(2,1)} fusion(bf16[16,256,1,128]{3,1,2,0:T(8,128)(2,1)} %fusion.21, bf16[256,1,128]{2,1,0:T(2,128)(2,1)S(1)} %get-tuple-element.34), kind=kLoop, calls=%fused_computation.40 | loop fusion | bytes 131072
  8.2 0.6 %fusion.19 = bf16[16,256,1,128]{3,1,2,0:T(8,128)(2,1)} fusion(bf16[16,256,1,128]{3,1,2,0:T(8,128)(2,1)} %fusion.20, bf16[256,1,128]{2,1,0:T(2,128)(2,1)S(1)} %get-tuple-element.33), kind=kLoop, calls=%fused_computation.38 | loop fusion | bytes 131072
  8.9 0.6 %fusion.18 = bf16[16,256,1,128]{3,1,2,0:T(8,128)(2,1)} fusion(bf16[16,256,1,128]{3,1,2,0:T(8,128)(2,1)} %fusion.19, bf16[256,1,128]{2,1,0:T(2,128)(2,1)S(1)} %get-tuple-element.32), kind=kLoop, calls=%fused_computation.36 | loop fusion | bytes 131072
  9.5 0.6 %fusion.17 = bf16[16,256,1,128]{3,1,2,0:T(8,128)(2,1)} fusion(bf16[16,256,1,128]{3,1,2,0:T(8,128)(2,1)} %fusion.18, bf16[256,1,128]{2,1,0:T(2,128)(2,1)S(1)} %get-tuple-element.31), kind=kLoop, calls=%fused_computation.34 | loop fusion | bytes 131072
  10.1 0.6 %fusion.16 = bf16[16,256,1,128]{3,1,2,0:T(8,128)(2,1)} fusion(bf16[16,256,1,128]{3,1,2,0:T(8,128)(2,1)} %fusion.17, bf16[256,1,128]{2,1,0:T(2,128)(2,1)S(1)} %get-tuple-element.30), kind=kLoop, calls=%fused_computation.32 | loop fusion | bytes 131072
  10.8 0.6 %fusion.15 = bf16[16,256,1,128]{3,1,2,0:T(8,128)(2,1)} fusion(bf16[16,256,1,128]{3,1,2,0:T(8,128)(2,1)} %fusion.16, bf16[256,1,128]{2,1,0:T(2,128)(2,1)S(1)} %get-tuple-element.29), kind=kLoop, calls=%fused_computation.30 | loop fusion | bytes 131072
  11.4 0.6 %fusion.14 = bf16[16,256,1,128]{3,1,2,0:T(8,128)(2,1)} fusion(bf16[16,256,1,128]{3,1,2,0:T(8,128)(2,1)} %fusion.15, bf16[256,1,128]{2,1,0:T(2,128)(2,1)S(1)} %get-tuple-element.28), kind=kLoop, calls=%fused_computation.28 | loop fusion | bytes 131072
  12.0 0.6 %fusion.13 = bf16[16,256,1,128]{3,1,2,0:T(8,128)(2,1)} fusion(bf16[16,256,1,128]{3,1,2,0:T(8,128)(2,1)} %fusion.14, bf16[256,1,128]{2,1,0:T(2,128)(2,1)S(1)} %get-tuple-element.27), kind=kLoop, calls=%fused_computation.26 | loop fusion | bytes 131072
  12.6 0.6 %fusion.12 = bf16[16,256,1,128]{3,1,2,0:T(8,128)(2,1)} fusion(bf16[16,256,1,128]{3,1,2,0:T(8,128)(2,1)} %fusion.13, bf16[256,1,128]{2,1,0:T(2,128)(2,1)S(1)} %get-tuple-element.26), kind=kLoop, calls=%fused_computation.24 | loop fusion | bytes 131072
  13.3 0.6 %fusion.11 = bf16[16,256,1,128]{3,1,2,0:T(8,128)(2,1)} fusion(bf16[16,256,1,128]{3,1,2,0:T(8,128)(2,1)} %fusion.12, bf16[256,1,128]{2,1,0:T(2,128)(2,1)S(1)} %get-tuple-element.25), kind=kLoop, calls=%fused_computation.22 | loop fusion | bytes 131072
  13.9 0.6 %fusion.10 = bf16[16,256,1,128]{3,1,2,0:T(8,128)(2,1)} fusion(bf16[16,256,1,128]{3,1,2,0:T(8,128)(2,1)} %fusion.11, bf16[256,1,128]{2,1,0:T(2,128)(2,1)S(1)} %get-tuple-element.24), kind=kLoop, calls=%fused_computation.20 | loop fusion | bytes 131072
  14.5 0.6 %fusion.9 = bf16[16,256,1,128]{3,1,2,0:T(8,128)(2,1)} fusion(bf16[16,256,1,128]{3,1,2,0:T(8,128)(2,1)} %fusion.10, bf16[256,1,128]{2,1,0:T(2,128)(2,1)S(1)} %get-tuple-element.17), kind=kLoop, calls=%fused_computation.18 | loop fusion | bytes 131072
  15.2 0.6 %fusion.8 = bf16[16,256,1,128]{3,1,2,0:T(8,128)(2,1)} fusion(bf16[16,256,1,128]{3,1,2,0:T(8,128)(2,1)} %fusion.9, bf16[256,1,128]{2,1,0:T(2,128)(2,1)S(1)} %get-tuple-element.16), kind=kLoop, calls=%fused_computation.16 | loop fusion | bytes 131072
  15.8 0.6 %fusion.7 = bf16[16,256,1,128]{3,1,2,0:T(8,128)(2,1)} fusion(bf16[16,256,1,128]{3,1,2,0:T(8,128)(2,1)} %fusion.8, bf16[256,1,128]{2,1,0:T(2,128)(2,1)S(1)} %get-tuple-element.15), kind=kLoop, calls=%fused_computation.14 | loop fusion | bytes 131072
  16.4 0.6 %fusion.6 = bf16[16,256,1,128]{3,1,2,0:T(8,128)(2,1)} fusion(bf16[16,256,1,128]{3,1,2,0:T(8,128)(2,1)} %fusion.7, bf16[256,1,128]{2,1,0:T(2,128)(2,1)S(1)} %get-tuple-element.14), kind=kLoop, calls=%fused_computation.12 | loop fusion | bytes 131072 | tf_op jit(solution)/shard_map/stack | solution.py:45
  17.1 0.0 copy-start.2
  17.1 0.0 copy-start.3
  17.1 0.0 copy-start.1
  17.1 6.8 %all-to-all-start = ((bf16[16,256,1,128]{3,1,2,0:T(8,128)(2,1)}), bf16[16,256,1,128]{3,1,2,0:T(8,128)(2,1)S(1)}, u32[]{:S(2)}, u32[]{:S(2)}) async-start(bf16[16,256,1,128]{3,1,2,0:T(8,128)(2,1)} %fusion.6), calls=%async_computation | async-start | bytes 2097152 | tf_op jit(solution)/shard_map/all_to_all | solution.py:45
  23.9 0.0 copy-done.2
  23.9 0.6 %dynamic_slice.13 = s32[1]{0:T(128)} dynamic-slice(s32[16]{0:T(128)S(1)} %copy-done.2, s32[]{:T(128)S(6)} %select_n.55), dynamic_slice_sizes={1} | dynamic-slice | bytes 12 | tf_op jit(solution)/shard_map/dynamic_slice | solution.py:43
  24.5 0.6 %iota_compare_fusion.3 = pred[128]{0:T(512)(128)(4,1)S(1)} fusion(s32[]{:T(128)} %bitcast.2), kind=kLoop, calls=%fused_computation.52 | loop fusion | flops 128 | bytes 132 | tf_op jit(solution)/shard_map/lt | solution.py:51
  25.1 0.0 copy-done.3
  25.1 0.1 fusion.5
  25.3 23.0 %all-to-all-done = bf16[16,256,1,128]{3,1,2,0:T(8,128)(2,1)S(1)} async-done(((bf16[16,256,1,128]{3,1,2,0:T(8,128)(2,1)}), bf16[16,256,1,128]{3,1,2,0:T(8,128)(2,1)S(1)}, u32[]{:S(2)}, u32[]{:S(2)}) %all-to-all-start) | async-done | bytes 1048608 | tf_op jit(solution)/shard_map/all_to_all | solution.py:45
  48.2 0.0 copy-done
  48.2 0.0 copy-done.1
  48.2 5.1 %fusion = f32[1024,128]{1,0:T(8,128)S(1)} fusion(s32[4096]{0:T(1024)S(1)} %bitcast.83, bf16[4096,128]{1,0:T(8,128)(2,1)S(1)} %bitcast.82, pred[128]{0:T(512)(128)(4,1)S(1)} %iota_compare_fusion.3, bf16[1,128,128]{2,1,0:T(8,128)(2,1)S(1)} %copy-done), kind=kOutput, calls=%fused_computation.2 | convolution fusion | flops 1213202432 | bytes 1622144 | tf_op jit(solution)/shard_map/while/body/eval_jaxpr/dot_general | solution.py:30
  53.4 0.6 gather_fusion
  54.0 0.1 bitcast_select_fusion
  54.0 2.4 %collective-permute-start = (f32[1,16,128]{2,1,0:T(8,128)S(1)}, f32[1,16,128]{2,1,0:T(8,128)S(1)}, u32[]{:S(2)}, u32[]{:S(2)}) collective-permute-start(f32[1,16,128]{2,1,0:T(8,128)S(1)} %constant_dynamic-slice_fusion), channel_id=1, source_target_pairs={{0,16},{16,0},{1,17},{17,1},{2,18},{18,2},{3,19},{19,3},{4,20},{20... | collective-permute-start | bytes 24584 | tf_op jit(solution)/shard_map/ppermute | solution.py:17
  56.5 1.0 %select_bitcast_fusion = f32[1,1,1024,128]{3,2,1,0:T(8,128)} fusion(f32[1024,128]{1,0:T(8,128)S(1)} %fusion, pred[1024]{0:T(1024)(128)(4,1)S(1)} %fusion.5), kind=kLoop, calls=%fused_computation.8 | loop fusion | flops 131072 | bytes 1049600 | tf_op jit(solution)/shard_map/broadcast_in_dim | solution.py:64
  57.4 0.0 collective-permute-done
  57.5 0.6 %dynamic-slice_add_fusion = f32[1,16,128]{2,1,0:T(8,128)} fusion(f32[1,16,128]{2,1,0:T(8,128)S(1)} %collective-permute-done, f32[1,32,128]{2,1,0:T(8,128)S(1)} %bitcast_select_fusion, s32[]{:T(128)S(6)} %select_n.61), kind=kLoop, calls=%fused_computation.45 | loop fusion | flops 2048 | bytes 24580 | tf_op jit(solution)/shard_map/add | solution.py:60
  (4 shorter events, 0.0 us)
Async XLA Ops:
  0.6 47.6 %copy-start = (bf16[1,128,128]{2,1,0:T(8,128)(2,1)S(1)}, bf16[1,128,128]{2,1,0:T(8,128)(2,1)}, u32[]{:S(2)}) copy-start(bf16[1,128,128]{2,1,0:T(8,128)(2,1)} %param.7) | copy-start | bytes 98308
  17.1 6.8 %copy-start.2 = (s32[16]{0:T(128)S(1)}, s32[16]{0:T(128)}, u32[]{:S(2)}) copy-start(s32[16]{0:T(128)} %param.8) | copy-start | bytes 196
  17.1 8.1 %copy-start.3 = (s32[1,32]{1,0:T(1,128)S(1)}, s32[1,32]{1,0:T(1,128)}, u32[]{:S(2)}) copy-start(s32[1,32]{1,0:T(1,128)} %param.9) | copy-start | bytes 388
  17.1 31.2 %copy-start.1 = (s32[1,4096]{1,0:T(1,128)S(1)}, s32[1,4096]{1,0:T(1,128)}, u32[]{:S(2)}) copy-start(s32[1,4096]{1,0:T(1,128)} %param.6) | copy-start | bytes 49156
  17.1 31.2 %all-to-all-start = ((bf16[16,256,1,128]{3,1,2,0:T(8,128)(2,1)}), bf16[16,256,1,128]{3,1,2,0:T(8,128)(2,1)S(1)}, u32[]{:S(2)}, u32[]{:S(2)}) async-start(bf16[16,256,1,128]{3,1,2,0:T(8,128)(2,1)} %fusion.6), calls=%async_computation | async-start | bytes 2097152 | tf_op jit(solution)/shard_map/all_to_all | solution.py:45
  54.0 3.4 %collective-permute-start = (f32[1,16,128]{2,1,0:T(8,128)S(1)}, f32[1,16,128]{2,1,0:T(8,128)S(1)}, u32[]{:S(2)}, u32[]{:S(2)}) collective-permute-start(f32[1,16,128]{2,1,0:T(8,128)S(1)} %constant_dynamic-slice_fusion), channel_id=1, source_target_pairs={{0,16},{16,0},{1,17},{17,1},{2,18},{18,2},{3,19},{19,3},{4,20},{20... | collective-permute-start | bytes 24584 | tf_op jit(solution)/shard_map/ppermute | solution.py:17
